TPU v7x, 256 devices: a 4x2x16 block of a 4x16x16 slice. The times are simulated.
256 devices in a mesh: grp: 2 (over y), row: 128 (over x, z, core).
Axes of the slice: x: 4, y: 2, z: 16, core: 2. Of those that a mesh axis runs over, the one named last changes fastest.
The devices are a block of a 4x16x16 slice.
Arguments:
- diag_blocks: float32 [65536, 512], P('row'), may hold values from -0.6 to 2.6
- lower_coupling: float32 [65536, 64], P('row'), may hold values from -0.3125 to 0.3125
- upper_coupling: float32 [65536, 64], P('row'), may hold values from -0.3125 to 0.3125
- right_sides: float32 [65536, 1024], P('row', 'grp'), parts along dimension 1, may hold values from -108 to 108
Outputs:
- solution: float32 [65536, 1024], P('row', 'grp'), parts along dimension 1
- res_norms: float32 [8, 1024], P(None, 'grp'), parts along dimension 1
There are 2 independent parts, one for each index of `grp`. A program takes and returns all parts, laid end to end along the dimension named above; an argument that names none is the same for every part. Nothing has to cross between parts.
All inputs are finite; a program needn't handle non-finite values.
Results may differ from a plain program's by a relative error of at most 0.0001.
Values sent between devices are 32-bit elements; how exact they have to be, the bound alone decides.
A program may use at most 64 MiB of HBM per device.

v0:
```python
import functools

import jax
import jax.numpy as jnp
from jax import lax
from jax.sharding import Mesh
from jax.sharding import PartitionSpec as P

SWEEPS = 8
ROW = ("row_0", "row_1", "row_2")


def extended(shard, sides, width):
    for axis, dim in sides:
        size, length = (lax.axis_size(axis), shard.shape[dim])
        up = [(i, (i + 1) % size) for i in range(size - 1)]
        down = [(j, i) for i, j in up]
        last = lax.slice_in_dim(shard, length - width, length, axis=dim)
        first = lax.slice_in_dim(shard, 0, width, axis=dim)
        before = lax.ppermute(last, axis, up)
        after = lax.ppermute(first, axis, down)
        shard = jnp.concatenate([before, shard, after], axis=dim)
    return shard


def one_axis_at_a_time(shard, axes):
    return functools.reduce(lax.psum, axes, shard)


def matmul(left, right):
    return jnp.dot(left, right, precision=lax.Precision.HIGHEST, preferred_element_type=jnp.float32)


def local(diag_blocks, lower_coupling, upper_coupling, right_sides):
    pivots = jnp.diagonal(diag_blocks)[:, None]
    width = lower_coupling.shape[1]
    solution = jnp.zeros_like(right_sides)
    partials = []
    for sweep_index in range(SWEEPS):
        padded = extended(solution, ((ROW, 0),), width)
        before = padded[:width]
        after = padded[padded.shape[0] - width :]
        images = (
            matmul(diag_blocks, solution)
            + matmul(lower_coupling, before)
            + matmul(upper_coupling, after)
        )
        residual = right_sides - images
        local_sums = jnp.sum(residual * residual, axis=0)
        solution = solution + residual / pivots
        partials.append(local_sums)
    res_norms = jnp.sqrt(one_axis_at_a_time(jnp.stack(partials), ROW))
    return (solution, res_norms)


def solution(mesh):
    finer = Mesh(
        mesh.devices.reshape(mesh.shape["grp"], 4, 16, 2), ("grp", "row_0", "row_1", "row_2")
    )
    placed = (P(ROW, None), P(ROW, None), P(ROW, None), P(ROW, "grp"))
    return jax.shard_map(
        local,
        mesh=finer,
        in_specs=placed,
        out_specs=(P(ROW, "grp"), P(None, "grp")),
        check_vma=False,
    )
```

profile of v0, /device:TPU:33, one launch (start us, length us, event | category | flops | bytes accessed | tf_op | source)
XLA Modules:
  0.0 208.7 jit_solution(10611569295517323340)
XLA Ops:
  0.6 0.0 copy-start
  0.7 22.5 %collective-permute-start.1 = (f32[64,512]{1,0:T(8,128)S(1)}, f32[64,512]{1,0:T(8,128)S(1)}, u32[]{:S(2)}, u32[]{:S(2)}) collective-permute-start(f32[64,512]{1,0:T(8,128)S(1)} %broadcast.16), channel_id=1, source_target_pairs={{1,0},{2,1},{3,2},{4,3},{5,4},{6,5},{7,6},{8,7},{9,8},{10,9},{11,1... | collective-permute-start | bytes 393224 | tf_op jit(solution)/shard_map/ppermute | solution.py:21
  23.2 2.0 collective-permute-start
  25.1 0.0 copy-start.1
  25.1 8.5 %gather_fusion = f32[512]{0:T(512)S(1)} fusion(f32[512,512]{1,0:T(8,128)} %param.4, s32[512]{0:T(512)S(1)} %bitcast.87), kind=kCustom, calls=%fused_computation | custom fusion | bytes 8192 | tf_op jit(solution)/shard_map/jit(diagonal)/cond/branch_0_fun/gather | solution.py:35
  33.6 0.0 copy-start.3
  33.6 0.1 multiply_reduce_fusion.8
  33.8 0.0 copy-start.2
  33.8 0.0 collective-permute-done.1
  33.8 1.0 fusion.24
  34.8 0.0 collective-permute-done
  34.9 0.0 copy-done.2
  34.9 1.2 multiply_reduce_fusion.7
  36.1 2.0 collective-permute-start.2
  38.1 1.9 fusion.25
  40.0 2.4 %collective-permute-start.3 = (f32[64,512]{1,0:T(8,128)S(1)}, f32[64,512]{1,0:T(8,128)S(1)}, u32[]{:S(2)}, u32[]{:S(2)}) collective-permute-start(f32[64,512]{1,0:T(8,128)S(1)} %get-tuple-element.30), channel_id=1, source_target_pairs={{1,0},{2,1},{3,2},{4,3},{5,4},{6,5},{7,6},{8,7},{9,8},{10,9},{11,1... | collective-permute-start | bytes 393224 | tf_op jit(solution)/shard_map/ppermute | solution.py:21
  42.4 0.0 collective-permute-done.2
  42.4 1.0 convolution_add_fusion.13
  43.4 2.8 %collective-permute-done.3 = f32[64,512]{1,0:T(8,128)S(1)} collective-permute-done((f32[64,512]{1,0:T(8,128)S(1)}, f32[64,512]{1,0:T(8,128)S(1)}, u32[]{:S(2)}, u32[]{:S(2)}) %collective-permute-start.3) | collective-permute-done | bytes 131104 | tf_op jit(solution)/shard_map/ppermute | solution.py:21
  46.3 1.2 multiply_reduce_fusion.6
  47.5 2.0 collective-permute-start.4
  49.5 1.9 fusion.26
  51.3 2.4 %collective-permute-start.5 = (f32[64,512]{1,0:T(8,128)S(1)}, f32[64,512]{1,0:T(8,128)S(1)}, u32[]{:S(2)}, u32[]{:S(2)}) collective-permute-start(f32[64,512]{1,0:T(8,128)S(1)} %get-tuple-element.28), channel_id=1, source_target_pairs={{1,0},{2,1},{3,2},{4,3},{5,4},{6,5},{7,6},{8,7},{9,8},{10,9},{11,1... | collective-permute-start | bytes 393224 | tf_op jit(solution)/shard_map/ppermute | solution.py:21
  53.8 0.0 collective-permute-done.4
  53.8 1.0 convolution_add_fusion.11
  54.8 2.8 %collective-permute-done.5 = f32[64,512]{1,0:T(8,128)S(1)} collective-permute-done((f32[64,512]{1,0:T(8,128)S(1)}, f32[64,512]{1,0:T(8,128)S(1)}, u32[]{:S(2)}, u32[]{:S(2)}) %collective-permute-start.5) | collective-permute-done | bytes 131104 | tf_op jit(solution)/shard_map/ppermute | solution.py:21
  57.7 1.2 multiply_reduce_fusion.5
  58.9 2.1 %collective-permute-start.6 = (f32[64,512]{1,0:T(8,128)S(1)}, f32[64,512]{1,0:T(8,128)S(1)}, u32[]{:S(2)}, u32[]{:S(2)}) collective-permute-start(f32[64,512]{1,0:T(8,128)S(1)} %get-tuple-element.27), channel_id=1, source_target_pairs={{0,1},{1,2},{2,3},{3,4},{4,5},{5,6},{6,7},{7,8},{8,9},{9,10},{10,1... | collective-permute-start | bytes 393224 | tf_op jit(solution)/shard_map/ppermute | solution.py:20
  61.0 1.9 fusion.27
  62.9 2.4 %collective-permute-start.7 = (f32[64,512]{1,0:T(8,128)S(1)}, f32[64,512]{1,0:T(8,128)S(1)}, u32[]{:S(2)}, u32[]{:S(2)}) collective-permute-start(f32[64,512]{1,0:T(8,128)S(1)} %get-tuple-element.26), channel_id=1, source_target_pairs={{1,0},{2,1},{3,2},{4,3},{5,4},{6,5},{7,6},{8,7},{9,8},{10,9},{11,1... | collective-permute-start | bytes 393224 | tf_op jit(solution)/shard_map/ppermute | solution.py:21
  65.3 0.0 collective-permute-done.6
  65.4 1.0 convolution_add_fusion.9
  66.4 2.8 %collective-permute-done.7 = f32[64,512]{1,0:T(8,128)S(1)} collective-permute-done((f32[64,512]{1,0:T(8,128)S(1)}, f32[64,512]{1,0:T(8,128)S(1)}, u32[]{:S(2)}, u32[]{:S(2)}) %collective-permute-start.7) | collective-permute-done | bytes 131104 | tf_op jit(solution)/shard_map/ppermute | solution.py:21
  69.2 1.2 multiply_reduce_fusion.4
  70.4 2.0 collective-permute-start.8
  72.4 1.9 fusion.28
  74.3 2.4 %collective-permute-start.9 = (f32[64,512]{1,0:T(8,128)S(1)}, f32[64,512]{1,0:T(8,128)S(1)}, u32[]{:S(2)}, u32[]{:S(2)}) collective-permute-start(f32[64,512]{1,0:T(8,128)S(1)} %get-tuple-element.24), channel_id=1, source_target_pairs={{1,0},{2,1},{3,2},{4,3},{5,4},{6,5},{7,6},{8,7},{9,8},{10,9},{11,1... | collective-permute-start | bytes 393224 | tf_op jit(solution)/shard_map/ppermute | solution.py:21
  76.7 0.0 collective-permute-done.8
  76.7 1.0 convolution_add_fusion.7
  77.8 2.8 %collective-permute-done.9 = f32[64,512]{1,0:T(8,128)S(1)} collective-permute-done((f32[64,512]{1,0:T(8,128)S(1)}, f32[64,512]{1,0:T(8,128)S(1)}, u32[]{:S(2)}, u32[]{:S(2)}) %collective-permute-start.9) | collective-permute-done | bytes 131104 | tf_op jit(solution)/shard_map/ppermute | solution.py:21
  80.6 1.2 multiply_reduce_fusion.3
  81.8 2.0 collective-permute-start.10
  83.8 1.9 fusion.29
  85.7 2.4 %collective-permute-start.11 = (f32[64,512]{1,0:T(8,128)S(1)}, f32[64,512]{1,0:T(8,128)S(1)}, u32[]{:S(2)}, u32[]{:S(2)}) collective-permute-start(f32[64,512]{1,0:T(8,128)S(1)} %get-tuple-element.22), channel_id=1, source_target_pairs={{1,0},{2,1},{3,2},{4,3},{5,4},{6,5},{7,6},{8,7},{9,8},{10,9},{11,1... | collective-permute-start | bytes 393224 | tf_op jit(solution)/shard_map/ppermute | solution.py:21
  88.1 0.0 collective-permute-done.10
  88.1 1.0 convolution_add_fusion.5
  89.1 2.8 %collective-permute-done.11 = f32[64,512]{1,0:T(8,128)S(1)} collective-permute-done((f32[64,512]{1,0:T(8,128)S(1)}, f32[64,512]{1,0:T(8,128)S(1)}, u32[]{:S(2)}, u32[]{:S(2)}) %collective-permute-start.11) | collective-permute-done | bytes 131104 | tf_op jit(solution)/shard_map/ppermute | solution.py:21
  92.0 1.2 multiply_reduce_fusion.2
  93.2 2.2 %collective-permute-start.12 = (f32[64,512]{1,0:T(8,128)S(1)}, f32[64,512]{1,0:T(8,128)S(1)}, u32[]{:S(2)}, u32[]{:S(2)}) collective-permute-start(f32[64,512]{1,0:T(8,128)S(1)} %get-tuple-element.21), channel_id=1, source_target_pairs={{0,1},{1,2},{2,3},{3,4},{4,5},{5,6},{6,7},{7,8},{8,9},{9,10},{10,1... | collective-permute-start | bytes 393224 | tf_op jit(solution)/shard_map/ppermute | solution.py:20
  95.4 1.9 fusion.30
  97.3 2.4 %collective-permute-start.13 = (f32[64,512]{1,0:T(8,128)S(1)}, f32[64,512]{1,0:T(8,128)S(1)}, u32[]{:S(2)}, u32[]{:S(2)}) collective-permute-start(f32[64,512]{1,0:T(8,128)S(1)} %get-tuple-element.20), channel_id=1, source_target_pairs={{1,0},{2,1},{3,2},{4,3},{5,4},{6,5},{7,6},{8,7},{9,8},{10,9},{11,1... | collective-permute-start | bytes 393224 | tf_op jit(solution)/shard_map/ppermute | solution.py:21
  99.7 1.0 convolution_add_fusion.3
  100.7 2.8 %collective-permute-done.13 = f32[64,512]{1,0:T(8,128)S(1)} collective-permute-done((f32[64,512]{1,0:T(8,128)S(1)}, f32[64,512]{1,0:T(8,128)S(1)}, u32[]{:S(2)}, u32[]{:S(2)}) %collective-permute-start.13) | collective-permute-done | bytes 131104 | tf_op jit(solution)/shard_map/ppermute | solution.py:21
  103.6 1.2 multiply_reduce_fusion.1
  104.8 2.0 collective-permute-start.14
  106.8 1.9 fusion.31
  108.6 2.4 %collective-permute-start.15 = (f32[64,512]{1,0:T(8,128)S(1)}, f32[64,512]{1,0:T(8,128)S(1)}, u32[]{:S(2)}, u32[]{:S(2)}) collective-permute-start(f32[64,512]{1,0:T(8,128)S(1)} %get-tuple-element.18), channel_id=1, source_target_pairs={{1,0},{2,1},{3,2},{4,3},{5,4},{6,5},{7,6},{8,7},{9,8},{10,9},{11,1... | collective-permute-start | bytes 393224 | tf_op jit(solution)/shard_map/ppermute | solution.py:21
  111.1 1.0 convolution_add_fusion.1
  112.1 2.8 %collective-permute-done.15 = f32[64,512]{1,0:T(8,128)S(1)} collective-permute-done((f32[64,512]{1,0:T(8,128)S(1)}, f32[64,512]{1,0:T(8,128)S(1)}, u32[]{:S(2)}, u32[]{:S(2)}) %collective-permute-start.15) | collective-permute-done | bytes 131104 | tf_op jit(solution)/shard_map/ppermute | solution.py:21
  115.0 2.2 %multiply_reduce_fusion = (f32[512]{0:T(512)S(1)}, f32[512,512]{1,0:T(8,128)}) fusion(f32[512,512]{1,0:T(8,128)S(1)} %get-tuple-element.5, f32[512]{0:T(512)S(1)} %gather_fusion, f32[512,512]{1,0:T(8,128)S(1)} %copy-done.3, f32[512,512]{0,1:T(8,128)S(1)} %convolution_add_fusion.1, f32[64,512]{1,0:T(8,128)S(1)} %collective-permute-done.15, ...), kind=kOutput, calls=%fused_computation.33 | convolution fusion | flops 202898944 | bytes 4460544 | tf_op jit(solution)/shard_map/dot_general | solution.py:31
  117.1 25.8 %psum.21 = f32[8,512]{1,0:T(8,128)S(1)} all-reduce(f32[8,512]{1,0:T(8,128)S(1)} %stack.35), channel_id=1, replica_groups=mesh['grp'=2,'row_0'=4,'row_1'=16,'row_2'=2] {'row_0'}, use_global_device_ids=true, to_apply=%region_9.10 | all-reduce | flops 4096 | bytes 32768 | tf_op jit(solution)/shard_map/psum | solution.py:27
  143.0 46.1 %psum.22 = f32[8,512]{1,0:T(8,128)S(1)} all-reduce(f32[8,512]{1,0:T(8,128)S(1)} %psum.21), channel_id=1, replica_groups=mesh['grp'=2,'row_0'=4,'row_1'=16,'row_2'=2] {'row_1'}, use_global_device_ids=true, to_apply=%region_10.11 | all-reduce | flops 4096 | bytes 32768 | tf_op jit(solution)/shard_map/psum | solution.py:27
  189.1 19.0 %psum.23 = f32[8,512]{1,0:T(8,128)S(1)} all-reduce(f32[8,512]{1,0:T(8,128)S(1)} %psum.22), channel_id=1, replica_groups=mesh['grp'=2,'row_0'=4,'row_1'=16,'row_2'=2] {'row_2'}, use_global_device_ids=true, to_apply=%region_11.12 | all-reduce | flops 4096 | bytes 32768 | tf_op jit(solution)/shard_map/psum | solution.py:27
  208.1 0.6 sqrt.3
  (15 shorter events, 0.2 us)
Async XLA Ops:
  0.6 33.2 %copy-start = (f32[512,64]{0,1:T(8,128)S(1)}, f32[512,64]{0,1:T(8,128)}, u32[]{:S(2)}) copy-start(f32[512,64]{0,1:T(8,128)} %param.6) | copy-start | bytes 393220
  0.7 33.1 %collective-permute-start.1 = (f32[64,512]{1,0:T(8,128)S(1)}, f32[64,512]{1,0:T(8,128)S(1)}, u32[]{:S(2)}, u32[]{:S(2)}) collective-permute-start(f32[64,512]{1,0:T(8,128)S(1)} %broadcast.16), channel_id=1, source_target_pairs={{1,0},{2,1},{3,2},{4,3},{5,4},{6,5},{7,6},{8,7},{9,8},{10,9},{11,1... | collective-permute-start | bytes 393224 | tf_op jit(solution)/shard_map/ppermute | solution.py:21
  23.2 11.7 %collective-permute-start = (f32[64,512]{1,0:T(8,128)S(1)}, f32[64,512]{1,0:T(8,128)S(1)}, u32[]{:S(2)}, u32[]{:S(2)}) collective-permute-start(f32[64,512]{1,0:T(8,128)S(1)} %broadcast.16), channel_id=1, source_target_pairs={{0,1},{1,2},{2,3},{3,4},{4,5},{5,6},{6,7},{7,8},{8,9},{9,10},{10,1... | collective-permute-start | bytes 393224 | tf_op jit(solution)/shard_map/ppermute | solution.py:20
  25.1 8.5 %copy-start.1 = (f32[512,512]{1,0:T(8,128)S(1)}, f32[512,512]{1,0:T(8,128)}, u32[]{:S(2)}) copy-start(f32[512,512]{1,0:T(8,128)} %param.4) | copy-start | bytes 3145732
  33.6 1.2 copy-start.3
  33.8 1.1 copy-start.2
  36.1 6.3 %collective-permute-start.2 = (f32[64,512]{1,0:T(8,128)S(1)}, f32[64,512]{1,0:T(8,128)S(1)}, u32[]{:S(2)}, u32[]{:S(2)}) collective-permute-start(f32[64,512]{1,0:T(8,128)S(1)} %get-tuple-element.31), channel_id=1, source_target_pairs={{0,1},{1,2},{2,3},{3,4},{4,5},{5,6},{6,7},{7,8},{8,9},{9,10},{10,1... | collective-permute-start | bytes 393224 | tf_op jit(solution)/shard_map/ppermute | solution.py:20
  40.0 6.3 %collective-permute-start.3 = (f32[64,512]{1,0:T(8,128)S(1)}, f32[64,512]{1,0:T(8,128)S(1)}, u32[]{:S(2)}, u32[]{:S(2)}) collective-permute-start(f32[64,512]{1,0:T(8,128)S(1)} %get-tuple-element.30), channel_id=1, source_target_pairs={{1,0},{2,1},{3,2},{4,3},{5,4},{6,5},{7,6},{8,7},{9,8},{10,9},{11,1... | collective-permute-start | bytes 393224 | tf_op jit(solution)/shard_map/ppermute | solution.py:21
  47.5 6.3 %collective-permute-start.4 = (f32[64,512]{1,0:T(8,128)S(1)}, f32[64,512]{1,0:T(8,128)S(1)}, u32[]{:S(2)}, u32[]{:S(2)}) collective-permute-start(f32[64,512]{1,0:T(8,128)S(1)} %get-tuple-element.29), channel_id=1, source_target_pairs={{0,1},{1,2},{2,3},{3,4},{4,5},{5,6},{6,7},{7,8},{8,9},{9,10},{10,1... | collective-permute-start | bytes 393224 | tf_op jit(solution)/shard_map/ppermute | solution.py:20
  51.3 6.3 %collective-permute-start.5 = (f32[64,512]{1,0:T(8,128)S(1)}, f32[64,512]{1,0:T(8,128)S(1)}, u32[]{:S(2)}, u32[]{:S(2)}) collective-permute-start(f32[64,512]{1,0:T(8,128)S(1)} %get-tuple-element.28), channel_id=1, source_target_pairs={{1,0},{2,1},{3,2},{4,3},{5,4},{6,5},{7,6},{8,7},{9,8},{10,9},{11,1... | collective-permute-start | bytes 393224 | tf_op jit(solution)/shard_map/ppermute | solution.py:21
  58.9 6.5 %collective-permute-start.6 = (f32[64,512]{1,0:T(8,128)S(1)}, f32[64,512]{1,0:T(8,128)S(1)}, u32[]{:S(2)}, u32[]{:S(2)}) collective-permute-start(f32[64,512]{1,0:T(8,128)S(1)} %get-tuple-element.27), channel_id=1, source_target_pairs={{0,1},{1,2},{2,3},{3,4},{4,5},{5,6},{6,7},{7,8},{8,9},{9,10},{10,1... | collective-permute-start | bytes 393224 | tf_op jit(solution)/shard_map/ppermute | solution.py:20
  62.9 6.3 %collective-permute-start.7 = (f32[64,512]{1,0:T(8,128)S(1)}, f32[64,512]{1,0:T(8,128)S(1)}, u32[]{:S(2)}, u32[]{:S(2)}) collective-permute-start(f32[64,512]{1,0:T(8,128)S(1)} %get-tuple-element.26), channel_id=1, source_target_pairs={{1,0},{2,1},{3,2},{4,3},{5,4},{6,5},{7,6},{8,7},{9,8},{10,9},{11,1... | collective-permute-start | bytes 393224 | tf_op jit(solution)/shard_map/ppermute | solution.py:21
  70.4 6.3 %collective-permute-start.8 = (f32[64,512]{1,0:T(8,128)S(1)}, f32[64,512]{1,0:T(8,128)S(1)}, u32[]{:S(2)}, u32[]{:S(2)}) collective-permute-start(f32[64,512]{1,0:T(8,128)S(1)} %get-tuple-element.25), channel_id=1, source_target_pairs={{0,1},{1,2},{2,3},{3,4},{4,5},{5,6},{6,7},{7,8},{8,9},{9,10},{10,1... | collective-permute-start | bytes 393224 | tf_op jit(solution)/shard_map/ppermute | solution.py:20
  74.3 6.3 %collective-permute-start.9 = (f32[64,512]{1,0:T(8,128)S(1)}, f32[64,512]{1,0:T(8,128)S(1)}, u32[]{:S(2)}, u32[]{:S(2)}) collective-permute-start(f32[64,512]{1,0:T(8,128)S(1)} %get-tuple-element.24), channel_id=1, source_target_pairs={{1,0},{2,1},{3,2},{4,3},{5,4},{6,5},{7,6},{8,7},{9,8},{10,9},{11,1... | collective-permute-start | bytes 393224 | tf_op jit(solution)/shard_map/ppermute | solution.py:21
  81.8 6.3 %collective-permute-start.10 = (f32[64,512]{1,0:T(8,128)S(1)}, f32[64,512]{1,0:T(8,128)S(1)}, u32[]{:S(2)}, u32[]{:S(2)}) collective-permute-start(f32[64,512]{1,0:T(8,128)S(1)} %get-tuple-element.23), channel_id=1, source_target_pairs={{0,1},{1,2},{2,3},{3,4},{4,5},{5,6},{6,7},{7,8},{8,9},{9,10},{10,1... | collective-permute-start | bytes 393224 | tf_op jit(solution)/shard_map/ppermute | solution.py:20
  85.7 6.3 %collective-permute-start.11 = (f32[64,512]{1,0:T(8,128)S(1)}, f32[64,512]{1,0:T(8,128)S(1)}, u32[]{:S(2)}, u32[]{:S(2)}) collective-permute-start(f32[64,512]{1,0:T(8,128)S(1)} %get-tuple-element.22), channel_id=1, source_target_pairs={{1,0},{2,1},{3,2},{4,3},{5,4},{6,5},{7,6},{8,7},{9,8},{10,9},{11,1... | collective-permute-start | bytes 393224 | tf_op jit(solution)/shard_map/ppermute | solution.py:21
  93.2 6.5 %collective-permute-start.12 = (f32[64,512]{1,0:T(8,128)S(1)}, f32[64,512]{1,0:T(8,128)S(1)}, u32[]{:S(2)}, u32[]{:S(2)}) collective-permute-start(f32[64,512]{1,0:T(8,128)S(1)} %get-tuple-element.21), channel_id=1, source_target_pairs={{0,1},{1,2},{2,3},{3,4},{4,5},{5,6},{6,7},{7,8},{8,9},{9,10},{10,1... | collective-permute-start | bytes 393224 | tf_op jit(solution)/shard_map/ppermute | solution.py:20
  97.3 6.3 %collective-permute-start.13 = (f32[64,512]{1,0:T(8,128)S(1)}, f32[64,512]{1,0:T(8,128)S(1)}, u32[]{:S(2)}, u32[]{:S(2)}) collective-permute-start(f32[64,512]{1,0:T(8,128)S(1)} %get-tuple-element.20), channel_id=1, source_target_pairs={{1,0},{2,1},{3,2},{4,3},{5,4},{6,5},{7,6},{8,7},{9,8},{10,9},{11,1... | collective-permute-start | bytes 393224 | tf_op jit(solution)/shard_map/ppermute | solution.py:21
  104.8 6.3 %collective-permute-start.14 = (f32[64,512]{1,0:T(8,128)S(1)}, f32[64,512]{1,0:T(8,128)S(1)}, u32[]{:S(2)}, u32[]{:S(2)}) collective-permute-start(f32[64,512]{1,0:T(8,128)S(1)} %get-tuple-element.19), channel_id=1, source_target_pairs={{0,1},{1,2},{2,3},{3,4},{4,5},{5,6},{6,7},{7,8},{8,9},{9,10},{10,1... | collective-permute-start | bytes 393224 | tf_op jit(solution)/shard_map/ppermute | solution.py:20
  108.6 6.3 %collective-permute-start.15 = (f32[64,512]{1,0:T(8,128)S(1)}, f32[64,512]{1,0:T(8,128)S(1)}, u32[]{:S(2)}, u32[]{:S(2)}) collective-permute-start(f32[64,512]{1,0:T(8,128)S(1)} %get-tuple-element.18), channel_id=1, source_target_pairs={{1,0},{2,1},{3,2},{4,3},{5,4},{6,5},{7,6},{8,7},{9,8},{10,9},{11,1... | collective-permute-start | bytes 393224 | tf_op jit(solution)/shard_map/ppermute | solution.py:21
where the time goes:
time: 210 us; the launch traced here: 209 us
  blocking collectives  90.9 us (43%)
  starting transfers between devices  55.6 us (26%)
  matrix products  31.8 us (15%)
  waiting for transfers between devices  19.8 us (9%)
  local copies, waits for them, and re-layouts  9.3 us (4%)
    psum x3, blocking collectives, one_axis_at_a_time(): return functools.reduce(lax.psum, axes, shard)  90.9 us
    ppermute x8, starting transfers between devices, extended(): after = lax.ppermute(first, axis, down)  39.6 us
    dot_general x23, matrix products, matmul(): jnp.dot(left, right, precision=lax.Precision.HIGHEST, preferred_element_t...  31.8 us
    ppermute x8, waiting for transfers between devices, extended(): after = lax.ppermute(first, axis, down)  19.8 us
    ppermute x8, starting transfers between devices, extended(): before = lax.ppermute(last, axis, up)  16 us
    gather x1, local copies, waits for them, and re-layouts, local(): pivots = jnp.diagonal(diag_blocks)[:, None]  8.46 us
  transfers between devices with their start and end apart: 16, of which 7 were waited for; matrix products, arithmetic and copies ran while one was open for 14% of the time, Pallas kernels for 0%

commit v1 on v0

v1 whole, which is shorter than its diff:
```python
import functools

import jax
import jax.numpy as jnp
from jax import lax
from jax.experimental import pallas as pl
from jax.experimental.pallas import tpu as pltpu
from jax.sharding import PartitionSpec as P

MESH = pl.DeviceIdType.MESH
SWEEPS = 8
DEPTH = 16
CORES = 2
CHUNKS = 2
F32 = jnp.float32
BF16 = jnp.bfloat16


def split(value):
    hi = value.astype(BF16)
    return hi, (value - hi.astype(F32)).astype(BF16)


def dot(left, right):
    return jnp.dot(left, right, preferred_element_type=F32)


def kernel(
    n, diag_hbm, lower_hbm, upper_hbm, rhs_hbm, x_acc, norms_ref,
    diag, lower, upper, rhs, recip, pivot, mats, edges, gmat_in, gmat_out, parts, ends_in, ends_out, inner_z,
    add_in, add_out, send_in, recv_in, send_out, recv_out, gsend_in, grecv_in, gsend_out, grecv_out,
    sums, early_plane, early_line, early_rows, late_plane, late_line,
    load_sem, si_sem, ri_sem, so_sem, ro_sem, g_sem,
    ap_send, ap_recv, bp_send, bp_recv, cp_send, cp_recv, al_send, al_recv, bl_send, bl_recv, know_a, know_b,
):
    width, size = lower_hbm.shape
    cols = rhs_hbm.shape[1]
    chunk = cols // CHUNKS
    last = SWEEPS - 1
    me = lax.axis_index("row")
    core = lax.rem(me, CORES)
    chip = lax.div(me, CORES)
    depth = lax.rem(chip, DEPTH)
    plane = lax.div(chip, DEPTH)
    planes = n // (CORES * DEPTH)
    members = planes * CORES
    place = plane * CORES + core
    near = me + 1 - 2 * core
    far = me - 1 + 2 * core
    has_far = jnp.logical_and(far >= 0, far < n)
    far_rows = pl.multiple_of(core * (size - width), width)
    near_rows = pl.multiple_of((1 - core) * (size - width), width)

    def at_place(other):
        return (lax.div(other, CORES) * DEPTH + depth) * CORES + lax.rem(other, CORES)

    def at_depth(other):
        return (plane * DEPTH + other) * CORES + core

    def signal(sem, target):
        pl.semaphore_signal(sem, inc=1, device_id={"row": target}, device_id_type=MESH)

    def remote(src, dst, send_sem, recv_sem, target):
        return pltpu.make_async_remote_copy(
            src_ref=src, dst_ref=dst, send_sem=send_sem, recv_sem=recv_sem,
            device_id={"row": target}, device_id_type=MESH,
        )

    slab = size // 4
    loads = []

    def load(src, dst):
        copy = pltpu.make_async_copy(src, dst, load_sem.at[len(loads)])
        copy.start()
        loads.append(copy)
        return copy

    diag_loads, rhs_loads = {}, {}
    for i in (0, 3):
        diag_loads[i] = load(diag_hbm.at[pl.ds(i * slab, slab)], diag.at[pl.ds(i * slab, slab)])
        rhs_loads[i] = load(rhs_hbm.at[pl.ds(i * slab, slab)], rhs.at[pl.ds(i * slab, slab)])
    lower_load = load(lower_hbm, lower)
    upper_load = load(upper_hbm, upper)
    for i in (1, 2):
        diag_loads[i] = load(diag_hbm.at[pl.ds(i * slab, slab)], diag.at[pl.ds(i * slab, slab)])
        rhs_loads[i] = load(rhs_hbm.at[pl.ds(i * slab, slab)], rhs.at[pl.ds(i * slab, slab)])

    barrier = pltpu.get_barrier_semaphore()
    for offset in range(1, members):
        signal(barrier, at_place(lax.rem(place + offset, members)))
    for offset in (1, 2, DEPTH - 2, DEPTH - 1):
        signal(barrier, at_depth(lax.rem(depth + offset, DEPTH)))

    @pl.when(has_far)
    def _():
        signal(barrier, far)

    @pl.when(jnp.logical_not(has_far))
    def _():
        recv_out[...] = jnp.zeros_like(recv_out)
        grecv_out[...] = jnp.zeros_like(grecv_out)

    add_in[...] = jnp.zeros_like(add_in)
    add_out[...] = jnp.zeros_like(add_out)

    mask = lax.broadcasted_iota(jnp.int32, (slab, slab), 0) == lax.broadcasted_iota(jnp.int32, (slab, slab), 1)

    def pivots(i):
        rows = pl.ds(i * slab, slab)
        block = diag[rows, pl.ds(i * slab, slab)]
        values = jnp.sum(jnp.where(mask, block, 0.0), axis=1, keepdims=True)
        pivot[rows, :] = jnp.broadcast_to(values, (slab, slab))
        first = 1.0 / values
        recip[rows, :] = jnp.broadcast_to(first + first * (1.0 - values * first), (slab, slab))

    def scale(block, rows):
        factor = recip[rows, :]
        return jnp.concatenate([block[:, j : j + slab] * factor for j in range(0, block.shape[1], slab)], axis=1)

    for i in (0, 3):
        diag_loads[i].wait()
        pivots(i)
    for i in (0, 3):
        rhs_loads[i].wait()
    for ch in range(CHUNKS):
        span = pl.ds(ch * chunk, chunk)
        near_slice, far_slice = pl.ds(near_rows, width), pl.ds(far_rows, width)
        send_out[0, ch] = scale(rhs[far_slice, span], far_slice)
        send_in[0, ch] = scale(rhs[near_slice, span], near_slice)

    @pl.when(has_far)
    def _():
        pl.semaphore_wait(barrier, members + 4)

    @pl.when(jnp.logical_not(has_far))
    def _():
        pl.semaphore_wait(barrier, members + 3)

    def near_copy(s, ch):
        return remote(send_in.at[s, ch], recv_in.at[s, ch], si_sem.at[s, ch], ri_sem.at[s, ch], near)

    def far_copy(s, ch):
        return remote(send_out.at[s, ch], recv_out.at[s, ch], so_sem.at[s, ch], ro_sem.at[s, ch], far)

    def g_copy_near():
        return remote(gsend_in, grecv_in, g_sem.at[0], g_sem.at[1], near)

    def g_copy_far():
        return remote(gsend_out, grecv_out, g_sem.at[2], g_sem.at[3], far)

    def if_far(action):
        @pl.when(has_far)
        def _():
            action()

    for ch in range(CHUNKS):
        if_far(lambda ch=ch: far_copy(0, ch).start())
        near_copy(0, ch).start()
    signal(know_a, at_depth(lax.rem(depth + 2, DEPTH)))
    signal(know_a, at_depth(lax.rem(depth + DEPTH - 2, DEPTH)))

    for i in (1, 2):
        diag_loads[i].wait()
        pivots(i)
    lower_load.wait()
    upper_load.wait()
    for i in range(4):
        rows = pl.ds(i * slab, slab)
        low, up = lower[:, rows].T, upper[:, rows].T
        to_near = jnp.where(core == 0, up, low)
        to_far = jnp.where(has_far, jnp.where(core == 0, low, up), 0.0)
        for position, block in enumerate((to_near, to_far)):
            twice = jnp.concatenate([block, block], axis=1) * (-recip[rows, :])
            hi, lo = split(twice)
            edges[rows, pl.ds(position * 2 * slab, slab)] = hi
            edges[rows, pl.ds(position * 2 * slab + slab, slab)] = lo

    def rejoin(rows, position):
        hi = edges[rows, pl.ds(position * 2 * slab, slab)].astype(F32)
        return hi + edges[rows, pl.ds(position * 2 * slab + slab, slab)].astype(F32)

    gsend_in[...] = rejoin(pl.ds(near_rows, width), 0)
    gsend_out[...] = rejoin(pl.ds(far_rows, width), 1)
    if_far(lambda: g_copy_far().start())
    g_copy_near().start()

    for i in range(4):
        rows = pl.ds(i * slab, slab)
        factor = -recip[rows, :]
        for j in range(4):
            block = diag[rows, pl.ds(j * slab, slab)]
            if i == j:
                block = jnp.where(mask, 0.0, block)
            hi, lo = split(block * factor)
            mats[rows, pl.ds(j * slab, slab)] = hi
            mats[rows, pl.ds(size + j * slab, slab)] = hi
            mats[rows, pl.ds(2 * size + j * slab, slab)] = lo

    for i in (1, 2):
        rhs_loads[i].wait()

    tile = 64

    def rows_sum(total):
        return jnp.sum(total, axis=0, keepdims=True)

    def keep(ch, r, value):
        hi, lo = split(value)
        parts[ch, pl.ds(r, tile), :] = hi
        parts[ch, pl.ds(size + r, tile), :] = lo

    def begin(ch):
        span = pl.ds(ch * chunk, chunk)
        total = jnp.zeros((8, chunk), F32)
        for r in range(0, size, tile):
            rows = pl.ds(r, tile)
            block = rhs[rows, span]
            total += jnp.sum((block * block).reshape(tile // 8, 8, chunk), axis=0)
            value = scale(block, rows)
            x_acc[rows, span] = value
            keep(ch, r, value)
        sums[0, :, span] = rows_sum(total)

    def advance(ch):
        low_high = parts[ch]
        inner_z[ch] = dot(mats[...], jnp.concatenate([low_high, low_high[:size]], axis=0))

    def echo(ch):
        for rows, gmat, add in ((near_rows, gmat_in, add_in), (far_rows, gmat_out, add_out)):
            hi = parts[ch, pl.ds(rows, width), :]
            lo = parts[ch, pl.ds(size + rows, width), :]
            add[ch] = dot(gmat[...], jnp.concatenate([hi, lo, hi, lo], axis=0))

    def take(ch, received, add, ends):
        hi, lo = split(received + add[ch])
        ends[ch] = jnp.concatenate([hi, lo, hi, lo], axis=0)

    def from_near(s, ch, send):
        near_copy(s, ch).wait_recv()
        take(ch, recv_in[s, ch], add_in, ends_in)
        if send:
            rows = pl.ds(far_rows, width)
            send_out[s + 1, ch] = inner_z[ch, rows, :] + dot(edges[rows, : 2 * slab], ends_in[ch])
            if_far(lambda: far_copy(s + 1, ch).start())

    def from_far(s, ch, send):
        if_far(lambda: far_copy(s, ch).wait_recv())
        take(ch, recv_out[s, ch], add_out, ends_out)
        if send:
            rows = pl.ds(near_rows, width)
            send_in[s + 1, ch] = inner_z[ch, rows, :] + dot(edges[rows, 2 * slab :], ends_out[ch])
            near_copy(s + 1, ch).start()

    def complete(s, ch, final):
        span = pl.ds(ch * chunk, chunk)
        inner_z[ch] += dot(edges[...], jnp.concatenate([ends_in[ch], ends_out[ch]], axis=0))
        total = jnp.zeros((8, chunk), F32)
        for r in range(0, size, tile):
            rows = pl.ds(r, tile)
            value = inner_z[ch, rows, :]
            x_acc[rows, span] += value
            if not final:
                keep(ch, r, value)
            factor = pivot[rows, :]
            residual = jnp.concatenate([value[:, j : j + slab] * factor for j in range(0, chunk, slab)], axis=1)
            total += jnp.sum((residual * residual).reshape(tile // 8, 8, chunk), axis=0)
        sums[s + 1, :, span] = rows_sum(total)

    for ch in range(CHUNKS):
        begin(ch)
        advance(ch)

    def sweep(s, carry):
        for ch in range(CHUNKS):
            from_near(s, ch, True)
        for ch in range(CHUNKS):
            from_far(s, ch, True)
            if ch == 0:

                if s == 0:
                    g_copy_near().wait_recv()
                    if_far(lambda: g_copy_far().wait_recv())
                    for source, target in ((grecv_in, gmat_in), (grecv_out, gmat_out)):
                        hi, lo = split(source[...])
                        target[:, :slab] = hi
                        target[:, slab:] = lo

            echo(ch)
            complete(s, ch, False)
            advance(ch)
        return carry

    for s in range(last - 1):
        sweep(s, 0)

    def spread(count, index, at, copy):
        for offset in range(1, count):
            copy(offset, lax.rem(index + offset, count))

    def early_a(offset, target_place):
        return remote(
            sums.at[target_place], early_plane.at[place], ap_send.at[offset], ap_recv.at[offset], at_place(target_place)
        )

    for offset in range(1, members):
        target_place = lax.rem(place + offset, members)

        @pl.when(target_place != last)
        def _(offset=offset, target_place=target_place):
            early_a(offset, target_place).start()

    pl.semaphore_wait(know_a, 2)
    signal(know_b, at_depth(lax.rem(depth + 4, DEPTH)))
    signal(know_b, at_depth(lax.rem(depth + DEPTH - 4, DEPTH)))

    for ch in range(CHUNKS):
        from_near(last - 1, ch, False)
    for ch in range(CHUNKS):
        from_far(last - 1, ch, False)
        complete(last - 1, ch, True)

    def late_a(offset):
        return remote(
            sums.at[last], late_plane.at[place], al_send.at[offset], al_recv.at[offset],
            at_place(lax.rem(place + offset, members)),
        )

    def line(buffer, send_sem, recv_sem, offset):
        return remote(
            buffer.at[depth], buffer.at[depth], send_sem.at[offset], recv_sem.at[offset],
            at_depth(lax.rem(depth + offset, DEPTH)),
        )

    def early_c(offset):
        return remote(
            early_rows.at[place], early_rows.at[place], cp_send.at[offset], cp_recv.at[offset],
            at_place(lax.rem(place + offset, members)),
        )

    def added(buffer, count):
        values = [buffer[i] for i in range(count)]
        while len(values) > 1:
            values = [values[i] + values[i + 1] for i in range(0, len(values), 2)]
        return values[0]

    for offset in range(1, members):
        late_a(offset).start()
    late_plane[place] = sums[last]
    pl.semaphore_wait(know_b, 2)

    @pl.when(place != last)
    def _():
        early_plane[place] = sums[place]
        for offset in range(1, members):
            early_a(offset, place).wait_recv()
        early_line[depth] = added(early_plane, members)
        for offset in range(1, DEPTH):
            line(early_line, bp_send, bp_recv, offset).start()

    for offset in range(1, members):
        late_a(offset).wait_recv()
    late_line[depth] = added(late_plane, members)
    for offset in range(1, DEPTH):
        line(late_line, bl_send, bl_recv, offset).start()

    @pl.when(place != last)
    def _():
        for offset in range(1, DEPTH):
            line(early_line, bp_send, bp_recv, offset).wait_recv()
        early_rows[place] = added(early_line, DEPTH)
        for offset in range(1, members):
            early_c(offset).start()

    for offset in range(1, DEPTH):
        line(late_line, bl_send, bl_recv, offset).wait_recv()
    norms_ref[last : last + 1, :] = jnp.sqrt(added(late_line, DEPTH))
    for offset in range(1, members):

        @pl.when(lax.rem(place + members - offset, members) != last)
        def _(offset=offset):
            early_c(offset).wait_recv()

    for i in range(last):
        norms_ref[i : i + 1, :] = jnp.sqrt(early_rows[i])

    for s in range(last):
        for ch in range(CHUNKS):
            near_copy(s, ch).wait_send()
            if_far(lambda s=s, ch=ch: far_copy(s, ch).wait_send())
    g_copy_near().wait_send()
    if_far(lambda: g_copy_far().wait_send())
    for offset in range(1, members):
        late_a(offset).wait_send()

        @pl.when(lax.rem(place + offset, members) != last)
        def _(offset=offset):
            early_a(offset, place).wait_send()

    for offset in range(1, DEPTH):
        line(late_line, bl_send, bl_recv, offset).wait_send()

    @pl.when(place != last)
    def _():
        for offset in range(1, DEPTH):
            line(early_line, bp_send, bp_recv, offset).wait_send()
        for offset in range(1, members):
            early_c(offset).wait_send()


def solution(mesh):
    n = mesh.shape["row"]
    members = n // DEPTH

    def step(diag_blocks, lower_coupling, upper_coupling, right_sides):
        size, width = lower_coupling.shape
        cols = right_sides.shape[1]
        chunk = cols // CHUNKS
        last = SWEEPS - 1
        dma = pltpu.SemaphoreType.DMA
        halo = pltpu.VMEM((last, CHUNKS, width, chunk), F32)
        square = pltpu.VMEM((width, 2 * width), F32)
        row = lambda count: pltpu.VMEM((count, 1, cols), F32)
        return pl.pallas_call(
            functools.partial(kernel, n),
            out_shape=(
                jax.ShapeDtypeStruct((size, cols), F32),
                jax.ShapeDtypeStruct((SWEEPS, cols), F32),
            ),
            in_specs=[pl.BlockSpec(memory_space=pltpu.HBM)] * 4,
            out_specs=(pl.BlockSpec(memory_space=pltpu.VMEM), pl.BlockSpec(memory_space=pltpu.VMEM)),
            scratch_shapes=[
                pltpu.VMEM((size, size), F32),
                pltpu.VMEM((width, size), F32),
                pltpu.VMEM((width, size), F32),
                pltpu.VMEM((size, cols), F32),
                pltpu.VMEM((size, size // 4), F32),
                pltpu.VMEM((size, size // 4), F32),
                pltpu.VMEM((size, 3 * size), BF16),
                pltpu.VMEM((size, 8 * width), BF16),
                pltpu.VMEM((width, 4 * width), BF16),
                pltpu.VMEM((width, 4 * width), BF16),
                pltpu.VMEM((CHUNKS, 2 * size, chunk), BF16),
                pltpu.VMEM((CHUNKS, 4 * width, chunk), BF16),
                pltpu.VMEM((CHUNKS, 4 * width, chunk), BF16),
                pltpu.VMEM((CHUNKS, size, chunk), F32),
                pltpu.VMEM((CHUNKS, width, chunk), F32),
                pltpu.VMEM((CHUNKS, width, chunk), F32),
                halo, halo, halo, halo,
                square, square, square, square,
                row(SWEEPS), row(members), row(DEPTH), row(members), row(members), row(DEPTH),
                dma((10,)),
                dma((last, CHUNKS)), dma((last, CHUNKS)), dma((last, CHUNKS)), dma((last, CHUNKS)), dma((4,)),
                dma((members,)), dma((members,)), dma((DEPTH,)), dma((DEPTH,)), dma((members,)), dma((members,)),
                dma((members,)), dma((members,)), dma((DEPTH,)), dma((DEPTH,)),
                pltpu.SemaphoreType.REGULAR, pltpu.SemaphoreType.REGULAR,
            ],
            compiler_params=pltpu.CompilerParams(
                collective_id=0, has_side_effects=True, vmem_limit_bytes=40 * 1024 * 1024
            ),
        )(*(
            pltpu.with_memory_space_constraint(array, pltpu.HBM)
            for array in (diag_blocks, lower_coupling.T, upper_coupling.T, right_sides)
        ))

    return jax.shard_map(
        step,
        mesh=mesh,
        in_specs=(P("row", None), P("row", None), P("row", None), P("row", "grp")),
        out_specs=(P("row", "grp"), P(None, "grp")),
        check_vma=False,
    )
```

time: 210 us -> 67.6 us (0.32)
  blocking collectives: 90.9 us -> 0 us
  Pallas kernels: 0 us -> 65.2 us
  starting transfers between devices: 55.6 us -> 0 us
  matrix products: 31.8 us -> 0 us
  waiting for transfers between devices: 19.8 us -> 0 us
  local copies, waits for them, and re-layouts: 9.3 us -> 1.58 us
    psum x3 -> x0, blocking collectives: 90.9 us -> none  [one_axis_at_a_time(): return functools.reduce(lax.psum, axes, shard)]
    pallas_call x0 -> x1, Pallas kernels: none -> 65.2 us  [step(): pl.pallas_call(functools.partial(kernel, n), out_shape=(jax.ShapeDtypeStr...]
    ppermute x16 -> x0, starting transfers between devices: 55.6 us -> none  [the longest x8 39.6 us: extended(): after = lax.ppermute(first, axis, down)]
    dot_general x23 -> x0, matrix products: 31.8 us -> none  [matmul(): jnp.dot(left, right, precision=lax.Precision.HIGHEST, preferred_element_t...]
    ppermute x16 -> x0, waiting for transfers between devices: 19.8 us -> none  [the longest x8 19.8 us: extended(): after = lax.ppermute(first, axis, down)]
    gather x1 -> x0, local copies, waits for them, and re-layouts: 8.46 us -> none  [local(): pivots = jnp.diagonal(diag_blocks)[:, None]]
  transfers between devices with their start and end apart: 16 -> 0, of which waited for: 7 -> 0; matrix products, arithmetic and copies ran while one was open for 14% -> 0% of each run, Pallas kernels for 0% -> 0%
where the time goes in v1:
time: 67.6 us; the launch traced here: 67.4 us
  Pallas kernels  65.2 us (96%)
  local copies, waits for them, and re-layouts  1.58 us (2%)
    pallas_call x1, Pallas kernels, step(): pl.pallas_call(functools.partial(kernel, n), out_shape=(jax.ShapeDtypeStr...  65.2 us
    unnamed x2, local copies, waits for them, and re-layouts  1.58 us

profile of v1, /device:TPU:33, one launch (start us, length us, event | category | flops | bytes accessed | tf_op | source)
XLA Modules:
  0.0 67.4 jit_solution(7184478951695539129)
XLA Ops:
  0.6 65.2 %shard_map.59 = (f32[512,512]{1,0:T(8,128)S(1)}, f32[8,512]{1,0:T(8,128)S(1)}) custom-call(f32[512,512]{1,0:T(8,128)} %diag_hbm.1, f32[64,512]{1,0:T(8,128)} %bitcast.2, f32[64,512]{1,0:T(8,128)} %bitcast.3, f32[512,512]{1,0:T(8,128)} %rhs_hbm.1), custom_call_target="tpu_custom_call" | custom-call | tf_op jit(solution)/shard_map/pallas_call | solution.py:423
  65.8 1.0 %copy.8 = f32[512,512]{1,0:T(8,128)} copy(f32[512,512]{1,0:T(8,128)S(1)} %get-tuple-element.4) | data formatting | bytes 2097152
  66.8 0.6 copy.9

commit v2 on v1

--- a/solution.py
+++ b/solution.py
@@ -37,6 +37,7 @@
     cols = rhs_hbm.shape[1]
     chunk = cols // CHUNKS
     last = SWEEPS - 1
+    early = SWEEPS - 2
     me = lax.axis_index("row")
     core = lax.rem(me, CORES)
     chip = lax.div(me, CORES)
@@ -270,59 +271,29 @@
         begin(ch)
         advance(ch)
 
-    def sweep(s, carry):
-        for ch in range(CHUNKS):
-            from_near(s, ch, True)
+    def take_squares():
+        g_copy_near().wait_recv()
+        if_far(lambda: g_copy_far().wait_recv())
+        for source, target in ((grecv_in, gmat_in), (grecv_out, gmat_out)):
+            hi, lo = split(source[...])
+            target[:, :slab] = hi
+            target[:, slab:] = lo
+
+    def sweep(s):
         for ch in range(CHUNKS):
             from_far(s, ch, True)
-            if ch == 0:
-
-                if s == 0:
-                    g_copy_near().wait_recv()
-                    if_far(lambda: g_copy_far().wait_recv())
-                    for source, target in ((grecv_in, gmat_in), (grecv_out, gmat_out)):
-                        hi, lo = split(source[...])
-                        target[:, :slab] = hi
-                        target[:, slab:] = lo
-
+            if ch > 0:
+                from_near(s + 1, ch - 1, s + 1 < last - 1)
+            elif s == 0:
+                take_squares()
             echo(ch)
             complete(s, ch, False)
             advance(ch)
-        return carry
-
-    for s in range(last - 1):
-        sweep(s, 0)
-
-    def spread(count, index, at, copy):
-        for offset in range(1, count):
-            copy(offset, lax.rem(index + offset, count))
+        from_near(s + 1, CHUNKS - 1, s + 1 < last - 1)
 
     def early_a(offset, target_place):
         return remote(
             sums.at[target_place], early_plane.at[place], ap_send.at[offset], ap_recv.at[offset], at_place(target_place)
-        )
-
-    for offset in range(1, members):
-        target_place = lax.rem(place + offset, members)
-
-        @pl.when(target_place != last)
-        def _(offset=offset, target_place=target_place):
-            early_a(offset, target_place).start()
-
-    pl.semaphore_wait(know_a, 2)
-    signal(know_b, at_depth(lax.rem(depth + 4, DEPTH)))
-    signal(know_b, at_depth(lax.rem(depth + DEPTH - 4, DEPTH)))
-
-    for ch in range(CHUNKS):
-        from_near(last - 1, ch, False)
-    for ch in range(CHUNKS):
-        from_far(last - 1, ch, False)
-        complete(last - 1, ch, True)
-
-    def late_a(offset):
-        return remote(
-            sums.at[last], late_plane.at[place], al_send.at[offset], al_recv.at[offset],
-            at_place(lax.rem(place + offset, members)),
         )
 
     def line(buffer, send_sem, recv_sem, offset):
@@ -331,6 +302,12 @@
             at_depth(lax.rem(depth + offset, DEPTH)),
         )
 
+    def late_a(offset):
+        return remote(
+            sums.at[pl.ds(early, SWEEPS - early)], late_plane.at[place], al_send.at[offset], al_recv.at[offset],
+            at_place(lax.rem(place + offset, members)),
+        )
+
     def early_c(offset):
         return remote(
             early_rows.at[place], early_rows.at[place], cp_send.at[offset], cp_recv.at[offset],
@@ -343,12 +320,26 @@
             values = [values[i] + values[i + 1] for i in range(0, len(values), 2)]
         return values[0]
 
-    for offset in range(1, members):
-        late_a(offset).start()
-    late_plane[place] = sums[last]
+    for ch in range(CHUNKS):
+        from_near(0, ch, True)
+    for s in range(early - 1):
+        sweep(s)
+
+    for offset in range(1, members):
+        target_place = lax.rem(place + offset, members)
+
+        @pl.when(target_place < early)
+        def _(offset=offset, target_place=target_place):
+            early_a(offset, target_place).start()
+
+    pl.semaphore_wait(know_a, 2)
+    signal(know_b, at_depth(lax.rem(depth + 4, DEPTH)))
+    signal(know_b, at_depth(lax.rem(depth + DEPTH - 4, DEPTH)))
+    for s in range(early - 1, last - 1):
+        sweep(s)
     pl.semaphore_wait(know_b, 2)
 
-    @pl.when(place != last)
+    @pl.when(place < early)
     def _():
         early_plane[place] = sums[place]
         for offset in range(1, members):
@@ -357,31 +348,13 @@
         for offset in range(1, DEPTH):
             line(early_line, bp_send, bp_recv, offset).start()
 
-    for offset in range(1, members):
-        late_a(offset).wait_recv()
-    late_line[depth] = added(late_plane, members)
-    for offset in range(1, DEPTH):
-        line(late_line, bl_send, bl_recv, offset).start()
-
-    @pl.when(place != last)
-    def _():
-        for offset in range(1, DEPTH):
-            line(early_line, bp_send, bp_recv, offset).wait_recv()
-        early_rows[place] = added(early_line, DEPTH)
-        for offset in range(1, members):
-            early_c(offset).start()
-
-    for offset in range(1, DEPTH):
-        line(late_line, bl_send, bl_recv, offset).wait_recv()
-    norms_ref[last : last + 1, :] = jnp.sqrt(added(late_line, DEPTH))
-    for offset in range(1, members):
-
-        @pl.when(lax.rem(place + members - offset, members) != last)
-        def _(offset=offset):
-            early_c(offset).wait_recv()
-
-    for i in range(last):
-        norms_ref[i : i + 1, :] = jnp.sqrt(early_rows[i])
+    for ch in range(CHUNKS):
+        from_far(last - 1, ch, False)
+        complete(last - 1, ch, True)
+
+    for offset in range(1, members):
+        late_a(offset).start()
+    late_plane[place] = sums[early:]
 
     for s in range(last):
         for ch in range(CHUNKS):
@@ -390,21 +363,62 @@
     g_copy_near().wait_send()
     if_far(lambda: g_copy_far().wait_send())
     for offset in range(1, members):
-        late_a(offset).wait_send()
-
-        @pl.when(lax.rem(place + offset, members) != last)
+
+        @pl.when(lax.rem(place + offset, members) < early)
         def _(offset=offset):
             early_a(offset, place).wait_send()
 
+    for offset in range(1, members):
+        late_a(offset).wait_recv()
+    late_line[depth] = added(late_plane, members)
     for offset in range(1, DEPTH):
-        line(late_line, bl_send, bl_recv, offset).wait_send()
-
-    @pl.when(place != last)
+        line(late_line, bl_send, bl_recv, offset).start()
+
+    @pl.when(place < early)
+    def _():
+        for offset in range(1, DEPTH):
+            line(early_line, bp_send, bp_recv, offset).wait_recv()
+        early_rows[place] = added(early_line, DEPTH)
+        for offset in range(1, members):
+            early_c(offset).start()
+
+    for offset in range(1, members):
+
+        @pl.when(lax.rem(place + members - offset, members) < early)
+        def _(offset=offset):
+            early_c(offset).wait_recv()
+
+    for i in range(early):
+        norms_ref[i : i + 1, :] = jnp.sqrt(early_rows[i])
+    for offset in range(1, members):
+        late_a(offset).wait_send()
+
+    @pl.when(place < early)
     def _():
         for offset in range(1, DEPTH):
             line(early_line, bp_send, bp_recv, offset).wait_send()
         for offset in range(1, members):
             early_c(offset).wait_send()
+
+    for offset in range(1, DEPTH):
+        line(late_line, bl_send, bl_recv, offset).wait_send()
+    for offset in range(1, DEPTH):
+        line(late_line, bl_send, bl_recv, offset).wait_recv()
+    total = added(late_line, DEPTH)
+    for i in range(early, SWEEPS):
+        norms_ref[i : i + 1, :] = jnp.sqrt(total[i - early])
+
+
+def put(x_ref, norms_ref, x_hbm, norms_hbm, sems):
+    size = x_ref.shape[0] // 4
+    copies = [pltpu.make_async_copy(norms_ref, norms_hbm, sems.at[4])]
+    for i in range(4):
+        rows = pl.ds(i * size, size)
+        copies.append(pltpu.make_async_copy(x_ref.at[rows], x_hbm.at[rows], sems.at[i]))
+    for copy in copies:
+        copy.start()
+    for copy in copies:
+        copy.wait()
 
 
 def solution(mesh):
@@ -420,7 +434,7 @@
         halo = pltpu.VMEM((last, CHUNKS, width, chunk), F32)
         square = pltpu.VMEM((width, 2 * width), F32)
         row = lambda count: pltpu.VMEM((count, 1, cols), F32)
-        return pl.pallas_call(
+        results = pl.pallas_call(
             functools.partial(kernel, n),
             out_shape=(
                 jax.ShapeDtypeStruct((size, cols), F32),
@@ -447,7 +461,8 @@
                 pltpu.VMEM((CHUNKS, width, chunk), F32),
                 halo, halo, halo, halo,
                 square, square, square, square,
-                row(SWEEPS), row(members), row(DEPTH), row(members), row(members), row(DEPTH),
+                row(SWEEPS), row(members), row(DEPTH), row(members),
+                pltpu.VMEM((members, 2, 1, cols), F32), pltpu.VMEM((DEPTH, 2, 1, cols), F32),
                 dma((10,)),
                 dma((last, CHUNKS)), dma((last, CHUNKS)), dma((last, CHUNKS)), dma((last, CHUNKS)), dma((4,)),
                 dma((members,)), dma((members,)), dma((DEPTH,)), dma((DEPTH,)), dma((members,)), dma((members,)),
@@ -461,6 +476,14 @@
             pltpu.with_memory_space_constraint(array, pltpu.HBM)
             for array in (diag_blocks, lower_coupling.T, upper_coupling.T, right_sides)
         ))
+        return pl.pallas_call(
+            put,
+            out_shape=tuple(jax.ShapeDtypeStruct(array.shape, F32) for array in results),
+            in_specs=[pl.BlockSpec(memory_space=pltpu.VMEM)] * 2,
+            out_specs=(pl.BlockSpec(memory_space=pltpu.HBM),) * 2,
+            scratch_shapes=[dma((5,))],
+            compiler_params=pltpu.CompilerParams(vmem_limit_bytes=1024 * 1024),
+        )(*results)
 
     return jax.shard_map(
         step,

time: 67.6 us -> 64.4 us (0.953)
  Pallas kernels: 65.2 us -> 63.5 us
  local copies, waits for them, and re-layouts: 1.58 us -> 0 us
    pallas_call x1, Pallas kernels: 65.2 us -> 62.5 us  [step(): pl.pallas_call(functools.partial(kernel, n), out_shape=(jax.ShapeDtypeStr...]
    unnamed x2 -> x0, local copies, waits for them, and re-layouts: 1.58 us -> none
    pallas_call x0 -> x1, Pallas kernels: none -> 1.01 us  [step(): pl.pallas_call(put, out_shape=tuple((jax.ShapeDtypeStruct(array.shape, F3...]
where the time goes in v2:
time: 64.4 us; the launch traced here: 64.3 us
  Pallas kernels  63.5 us (99%)
  between operations  0.8 us (1%)
    pallas_call x1, Pallas kernels, step(): pl.pallas_call(functools.partial(kernel, n), out_shape=(jax.ShapeDtypeStr...  62.5 us

profile of v2, /device:TPU:33, one launch (start us, length us, event | category | flops | bytes accessed | tf_op | source)
XLA Modules:
  0.0 64.3 jit_solution(1632631877907271204)
XLA Ops:
  0.6 62.5 %shard_map.59 = (f32[512,512]{1,0:T(8,128)S(1)}, f32[8,512]{1,0:T(8,128)S(1)}) custom-call(f32[512,512]{1,0:T(8,128)} %diag_hbm.1, f32[64,512]{1,0:T(8,128)} %bitcast.2, f32[64,512]{1,0:T(8,128)} %bitcast.3, f32[512,512]{1,0:T(8,128)} %rhs_hbm.1), custom_call_target="tpu_custom_call" | custom-call | tf_op jit(solution)/shard_map/pallas_call | solution.py:437
  63.1 1.0 %shard_map.60 = (f32[512,512]{1,0:T(8,128)}, f32[8,512]{1,0:T(8,128)}) custom-call(f32[512,512]{1,0:T(8,128)S(1)} %get-tuple-element.4.x_ref, f32[8,512]{1,0:T(8,128)S(1)} %get-tuple-element.5.norms_ref), custom_call_target="tpu_custom_call" | custom-call | tf_op jit(solution)/shard_map/pallas_call | solution.py:479

commit v3 on v2

--- a/solution.py
+++ b/solution.py
@@ -224,7 +224,9 @@
 
     def advance(ch):
         low_high = parts[ch]
-        inner_z[ch] = dot(mats[...], jnp.concatenate([low_high, low_high[:size]], axis=0))
+        right = jnp.concatenate([low_high, low_high[:size]], axis=0)
+        for r in range(0, size, size // 2):
+            inner_z[ch, pl.ds(r, size // 2), :] = dot(mats[pl.ds(r, size // 2), :], right)
 
     def echo(ch):
         for rows, gmat, add in ((near_rows, gmat_in, add_in), (far_rows, gmat_out, add_out)):
@@ -254,7 +256,9 @@
 
     def complete(s, ch, final):
         span = pl.ds(ch * chunk, chunk)
-        inner_z[ch] += dot(edges[...], jnp.concatenate([ends_in[ch], ends_out[ch]], axis=0))
+        right = jnp.concatenate([ends_in[ch], ends_out[ch]], axis=0)
+        for r in range(0, size, size // 2):
+            inner_z[ch, pl.ds(r, size // 2), :] += dot(edges[pl.ds(r, size // 2), :], right)
         total = jnp.zeros((8, chunk), F32)
         for r in range(0, size, tile):
             rows = pl.ds(r, tile)

time: 64.4 us -> 60.9 us (0.946)
  Pallas kernels: 63.5 us -> 60.2 us
    pallas_call x1, Pallas kernels: 62.5 us -> 59.2 us  [step(): pl.pallas_call(functools.partial(kernel, n), out_shape=(jax.ShapeDtypeStr...]
where the time goes in v3:
time: 60.9 us; the launch traced here: 60.8 us
  Pallas kernels  60.2 us (99%)
  between operations  0.64 us (1%)
    pallas_call x1, Pallas kernels, step(): pl.pallas_call(functools.partial(kernel, n), out_shape=(jax.ShapeDtypeStr...  59.2 us

profile of v3, /device:TPU:33, one launch (start us, length us, event | category | flops | bytes accessed | tf_op | source)
XLA Modules:
  0.0 60.8 jit_solution(14400203515475950796)
XLA Ops:
  0.6 59.2 %shard_map.59 = (f32[512,512]{1,0:T(8,128)S(1)}, f32[8,512]{1,0:T(8,128)S(1)}) custom-call(f32[512,512]{1,0:T(8,128)} %diag_hbm.1, f32[64,512]{1,0:T(8,128)} %bitcast.2, f32[64,512]{1,0:T(8,128)} %bitcast.3, f32[512,512]{1,0:T(8,128)} %rhs_hbm.1), custom_call_target="tpu_custom_call" | custom-call | tf_op jit(solution)/shard_map/pallas_call | solution.py:441
  59.8 1.0 %shard_map.60 = (f32[512,512]{1,0:T(8,128)}, f32[8,512]{1,0:T(8,128)}) custom-call(f32[512,512]{1,0:T(8,128)S(1)} %get-tuple-element.4.x_ref, f32[8,512]{1,0:T(8,128)S(1)} %get-tuple-element.5.norms_ref), custom_call_target="tpu_custom_call" | custom-call | tf_op jit(solution)/shard_map/pallas_call | solution.py:483

commit v4 on v3

--- a/solution.py
+++ b/solution.py
@@ -257,18 +257,19 @@
     def complete(s, ch, final):
         span = pl.ds(ch * chunk, chunk)
         right = jnp.concatenate([ends_in[ch], ends_out[ch]], axis=0)
-        for r in range(0, size, size // 2):
-            inner_z[ch, pl.ds(r, size // 2), :] += dot(edges[pl.ds(r, size // 2), :], right)
         total = jnp.zeros((8, chunk), F32)
-        for r in range(0, size, tile):
-            rows = pl.ds(r, tile)
-            value = inner_z[ch, rows, :]
-            x_acc[rows, span] += value
-            if not final:
-                keep(ch, r, value)
-            factor = pivot[rows, :]
-            residual = jnp.concatenate([value[:, j : j + slab] * factor for j in range(0, chunk, slab)], axis=1)
-            total += jnp.sum((residual * residual).reshape(tile // 8, 8, chunk), axis=0)
+        for start in range(0, size, size // 2):
+            half = pl.ds(start, size // 2)
+            block = inner_z[ch, half, :] + dot(edges[half, :], right)
+            for r in range(0, size // 2, tile):
+                rows = pl.ds(start + r, tile)
+                value = block[r : r + tile]
+                x_acc[rows, span] += value
+                if not final:
+                    keep(ch, start + r, value)
+                factor = pivot[rows, :]
+                residual = jnp.concatenate([value[:, j : j + slab] * factor for j in range(0, chunk, slab)], axis=1)
+                total += jnp.sum((residual * residual).reshape(tile // 8, 8, chunk), axis=0)
         sums[s + 1, :, span] = rows_sum(total)
 
     for ch in range(CHUNKS):
@@ -306,11 +307,26 @@
             at_depth(lax.rem(depth + offset, DEPTH)),
         )
 
-    def late_a(offset):
+    def late_a(i, offset):
         return remote(
-            sums.at[pl.ds(early, SWEEPS - early)], late_plane.at[place], al_send.at[offset], al_recv.at[offset],
+            sums.at[early + i], late_plane.at[i, place], al_send.at[i, offset], al_recv.at[i, offset],
             at_place(lax.rem(place + offset, members)),
         )
+
+    def late_b(i, offset):
+        return line(late_line.at[i], bl_send.at[i], bl_recv.at[i], offset)
+
+    def late_row(i):
+        for offset in range(1, members):
+            late_a(i, offset).start()
+        late_plane[i, place] = sums[early + i]
+
+    def late_sum(i):
+        for offset in range(1, members):
+            late_a(i, offset).wait_recv()
+        late_line[i, depth] = added(late_plane.at[i], members)
+        for offset in range(1, DEPTH):
+            late_b(i, offset).start()
 
     def early_c(offset):
         return remote(
@@ -341,6 +357,7 @@
     signal(know_b, at_depth(lax.rem(depth + DEPTH - 4, DEPTH)))
     for s in range(early - 1, last - 1):
         sweep(s)
+    late_row(0)
     pl.semaphore_wait(know_b, 2)
 
     @pl.when(place < early)
@@ -356,9 +373,7 @@
         from_far(last - 1, ch, False)
         complete(last - 1, ch, True)
 
-    for offset in range(1, members):
-        late_a(offset).start()
-    late_plane[place] = sums[early:]
+    late_row(1)
 
     for s in range(last):
         for ch in range(CHUNKS):
@@ -372,11 +387,8 @@
         def _(offset=offset):
             early_a(offset, place).wait_send()
 
-    for offset in range(1, members):
-        late_a(offset).wait_recv()
-    late_line[depth] = added(late_plane, members)
-    for offset in range(1, DEPTH):
-        line(late_line, bl_send, bl_recv, offset).start()
+    for i in range(SWEEPS - early):
+        late_sum(i)
 
     @pl.when(place < early)
     def _():
@@ -394,8 +406,9 @@
 
     for i in range(early):
         norms_ref[i : i + 1, :] = jnp.sqrt(early_rows[i])
-    for offset in range(1, members):
-        late_a(offset).wait_send()
+    for i in range(SWEEPS - early):
+        for offset in range(1, members):
+            late_a(i, offset).wait_send()
 
     @pl.when(place < early)
     def _():
@@ -404,13 +417,13 @@
         for offset in range(1, members):
             early_c(offset).wait_send()
 
-    for offset in range(1, DEPTH):
-        line(late_line, bl_send, bl_recv, offset).wait_send()
-    for offset in range(1, DEPTH):
-        line(late_line, bl_send, bl_recv, offset).wait_recv()
-    total = added(late_line, DEPTH)
-    for i in range(early, SWEEPS):
-        norms_ref[i : i + 1, :] = jnp.sqrt(total[i - early])
+    for i in range(SWEEPS - early):
+        for offset in range(1, DEPTH):
+            late_b(i, offset).wait_send()
+    for i in range(SWEEPS - early):
+        for offset in range(1, DEPTH):
+            late_b(i, offset).wait_recv()
+        norms_ref[early + i : early + i + 1, :] = jnp.sqrt(added(late_line.at[i], DEPTH))
 
 
 def put(x_ref, norms_ref, x_hbm, norms_hbm, sems):
@@ -466,11 +479,11 @@
                 halo, halo, halo, halo,
                 square, square, square, square,
                 row(SWEEPS), row(members), row(DEPTH), row(members),
-                pltpu.VMEM((members, 2, 1, cols), F32), pltpu.VMEM((DEPTH, 2, 1, cols), F32),
+                pltpu.VMEM((2, members, 1, cols), F32), pltpu.VMEM((2, DEPTH, 1, cols), F32),
                 dma((10,)),
                 dma((last, CHUNKS)), dma((last, CHUNKS)), dma((last, CHUNKS)), dma((last, CHUNKS)), dma((4,)),
                 dma((members,)), dma((members,)), dma((DEPTH,)), dma((DEPTH,)), dma((members,)), dma((members,)),
-                dma((members,)), dma((members,)), dma((DEPTH,)), dma((DEPTH,)),
+                dma((2, members)), dma((2, members)), dma((2, DEPTH)), dma((2, DEPTH)),
                 pltpu.SemaphoreType.REGULAR, pltpu.SemaphoreType.REGULAR,
             ],
             compiler_params=pltpu.CompilerParams(

time: 60.9 us -> 60.3 us (level)
    pallas_call x1, Pallas kernels: 59.2 us -> 58.5 us  [step(): pl.pallas_call(functools.partial(kernel, n), out_shape=(jax.ShapeDtypeStr...]
where the time goes in v4:
time: 60.3 us; the launch traced here: 60.2 us
  Pallas kernels  59.6 us (99%)
  between operations  0.64 us (1%)
    pallas_call x1, Pallas kernels, step(): pl.pallas_call(functools.partial(kernel, n), out_shape=(jax.ShapeDtypeStr...  58.5 us

profile of v4, /device:TPU:33, one launch (start us, length us, event | category | flops | bytes accessed | tf_op | source)
XLA Modules:
  0.0 60.2 jit_solution(11263134775880588716)
XLA Ops:
  0.6 58.5 %shard_map.59 = (f32[512,512]{1,0:T(8,128)S(1)}, f32[8,512]{1,0:T(8,128)S(1)}) custom-call(f32[512,512]{1,0:T(8,128)} %diag_hbm.1, f32[64,512]{1,0:T(8,128)} %bitcast.2, f32[64,512]{1,0:T(8,128)} %bitcast.3, f32[512,512]{1,0:T(8,128)} %rhs_hbm.1), custom_call_target="tpu_custom_call" | custom-call | tf_op jit(solution)/shard_map/pallas_call | solution.py:454
  59.2 1.0 %shard_map.60 = (f32[512,512]{1,0:T(8,128)}, f32[8,512]{1,0:T(8,128)}) custom-call(f32[512,512]{1,0:T(8,128)S(1)} %get-tuple-element.4.x_ref, f32[8,512]{1,0:T(8,128)S(1)} %get-tuple-element.5.norms_ref), custom_call_target="tpu_custom_call" | custom-call | tf_op jit(solution)/shard_map/pallas_call | solution.py:496

commit v5 on v4

--- a/solution.py
+++ b/solution.py
@@ -342,7 +342,11 @@
 
     for ch in range(CHUNKS):
         from_near(0, ch, True)
-    for s in range(early - 1):
+    sweep(0)
+    pl.semaphore_wait(know_a, 2)
+    signal(know_b, at_depth(lax.rem(depth + 4, DEPTH)))
+    signal(know_b, at_depth(lax.rem(depth + DEPTH - 4, DEPTH)))
+    for s in range(1, early - 1):
         sweep(s)
 
     for offset in range(1, members):
@@ -352,9 +356,6 @@
         def _(offset=offset, target_place=target_place):
             early_a(offset, target_place).start()
 
-    pl.semaphore_wait(know_a, 2)
-    signal(know_b, at_depth(lax.rem(depth + 4, DEPTH)))
-    signal(know_b, at_depth(lax.rem(depth + DEPTH - 4, DEPTH)))
     for s in range(early - 1, last - 1):
         sweep(s)
     late_row(0)

time: 60.3 us -> 59 us (0.978)
  Pallas kernels: 59.6 us -> 58.3 us
    pallas_call x1, Pallas kernels: 58.5 us -> 57.2 us  [step(): pl.pallas_call(functools.partial(kernel, n), out_shape=(jax.ShapeDtypeStr...]
where the time goes in v5:
time: 59 us; the launch traced here: 58.9 us
  Pallas kernels  58.3 us (99%)
  between operations  0.64 us (1%)
    pallas_call x1, Pallas kernels, step(): pl.pallas_call(functools.partial(kernel, n), out_shape=(jax.ShapeDtypeStr...  57.2 us

profile of v5, /device:TPU:33, one launch (start us, length us, event | category | flops | bytes accessed | tf_op | source)
XLA Modules:
  0.0 58.9 jit_solution(17519063975405517075)
XLA Ops:
  0.6 57.2 %shard_map.59 = (f32[512,512]{1,0:T(8,128)S(1)}, f32[8,512]{1,0:T(8,128)S(1)}) custom-call(f32[512,512]{1,0:T(8,128)} %diag_hbm.1, f32[64,512]{1,0:T(8,128)} %bitcast.2, f32[64,512]{1,0:T(8,128)} %bitcast.3, f32[512,512]{1,0:T(8,128)} %rhs_hbm.1), custom_call_target="tpu_custom_call" | custom-call | tf_op jit(solution)/shard_map/pallas_call | solution.py:455
  57.9 1.0 %shard_map.60 = (f32[512,512]{1,0:T(8,128)}, f32[8,512]{1,0:T(8,128)}) custom-call(f32[512,512]{1,0:T(8,128)S(1)} %get-tuple-element.4.x_ref, f32[8,512]{1,0:T(8,128)S(1)} %get-tuple-element.5.norms_ref), custom_call_target="tpu_custom_call" | custom-call | tf_op jit(solution)/shard_map/pallas_call | solution.py:497

commit v6 on v5

--- a/solution.py
+++ b/solution.py
@@ -286,10 +286,10 @@
 
     def sweep(s):
         for ch in range(CHUNKS):
-            from_far(s, ch, True)
             if ch > 0:
                 from_near(s + 1, ch - 1, s + 1 < last - 1)
-            elif s == 0:
+            from_far(s, ch, True)
+            if ch == 0 and s == 0:
                 take_squares()
             echo(ch)
             complete(s, ch, False)

time: 59 us -> 59.1 us (level)
  no operation moved by 1% of the time
where the time goes in v6:
time: 59.1 us; the launch traced here: 58.9 us
  Pallas kernels  58.3 us (99%)
  between operations  0.64 us (1%)
    pallas_call x1, Pallas kernels, step(): pl.pallas_call(functools.partial(kernel, n), out_shape=(jax.ShapeDtypeStr...  57.3 us

profile of v6, /device:TPU:33, one launch (start us, length us, event | category | flops | bytes accessed | tf_op | source)
XLA Modules:
  0.0 58.9 jit_solution(3036271352282735476)
XLA Ops:
  0.6 57.3 %shard_map.59 = (f32[512,512]{1,0:T(8,128)S(1)}, f32[8,512]{1,0:T(8,128)S(1)}) custom-call(f32[512,512]{1,0:T(8,128)} %diag_hbm.1, f32[64,512]{1,0:T(8,128)} %bitcast.2, f32[64,512]{1,0:T(8,128)} %bitcast.3, f32[512,512]{1,0:T(8,128)} %rhs_hbm.1), custom_call_target="tpu_custom_call" | custom-call | tf_op jit(solution)/shard_map/pallas_call | solution.py:455
  57.9 1.0 %shard_map.60 = (f32[512,512]{1,0:T(8,128)}, f32[8,512]{1,0:T(8,128)}) custom-call(f32[512,512]{1,0:T(8,128)S(1)} %get-tuple-element.4.x_ref, f32[8,512]{1,0:T(8,128)S(1)} %get-tuple-element.5.norms_ref), custom_call_target="tpu_custom_call" | custom-call | tf_op jit(solution)/shard_map/pallas_call | solution.py:497
